TPU v7x, 32 devices: a whole 2x2x4 slice. The times are simulated.
32 devices in a mesh: snp: 8 (over z, y), probe: 4 (over x, core).
Axes of the slice: x: 2, y: 2, z: 4, core: 2. Of those that a mesh axis runs over, the one named last changes fastest.
Arguments:
- dosage: bfloat16 [256, 16384], P(None, 'snp'), may hold values from 0 to 2, as said below
- allele_freq: float32 [16384], P('snp'), may hold values from 0.05 to 0.5
- probes: bfloat16 [32, 256], P('probe'), may hold values from -1 to 1, as said below
Outputs:
- kin_twice: float32 [32, 256], P('probe', 'snp')
- forms: float32 [2, 32], P(None, 'probe')
- estimates: float32 [2], replicated
Inputs may be any that keep to these rules, and one draw needn't show every extreme that they name: `dosage`: whole dosages. `probes`: every entry is -1 or 1.
All inputs are finite; a program needn't handle non-finite values.
Results may differ from a plain program's by a relative error of at most 0.0032.
Values may be sent and summed in bfloat16 or wider, within the bound.
No kernel may reach another device: no remote copies, remote signals or barrier semaphores. Data moves between devices by JAX's collectives and lax.ppermute only.
A program may use at most 64 MiB of HBM per device.

v0:
```python
import jax
import jax.numpy as jnp
from jax import lax
from jax.sharding import PartitionSpec as P


def apply_columns(vectors, standard):
    projected = jnp.dot(vectors, standard, preferred_element_type=jnp.float32).astype(jnp.bfloat16)
    return lax.dot_general(
        projected, standard, (((1,), (1,)), ((), ())), preferred_element_type=jnp.float32
    )


def body(dosage, allele_freq, probes):
    snp_count = lax.axis_size("snp")
    columns = dosage.shape[1] * snp_count
    owned = dosage.shape[0] // snp_count
    samples_all = dosage.shape[0]
    probes_all = probes.shape[0] * lax.axis_size("probe")
    scaling = lax.rsqrt(2.0 * allele_freq * (1.0 - allele_freq))
    standard = ((dosage.astype(jnp.float32) - 2.0 * allele_freq) * scaling).astype(jnp.bfloat16)
    start = lax.axis_index("snp") * owned
    signs_owned = lax.dynamic_slice_in_dim(probes, start, owned, 1).astype(jnp.float32)
    partial_once = apply_columns(probes, standard)
    summed = lax.psum(partial_once, "snp") / columns
    kin_owned = lax.dynamic_slice_in_dim(summed, start, owned, 1)
    kin_round = summed.astype(jnp.bfloat16)
    local_first = jnp.sum(signs_owned * kin_owned, axis=1) / samples_all
    form_first = lax.psum(local_first, "snp")
    partial_twice = apply_columns(kin_round, standard)
    kin_twice = lax.psum_scatter(partial_twice, "snp", scatter_dimension=1, tiled=True) / columns
    local_second = jnp.sum(signs_owned * kin_twice, axis=1) / samples_all
    form_second = lax.psum(local_second, "snp")
    forms = jnp.stack([form_first, form_second])
    estimates = lax.psum(jnp.sum(forms, axis=1), "probe") / probes_all
    return (kin_twice, forms, estimates)


def solution(mesh):
    placed = (P(None, "snp"), P("snp"), P("probe", None))
    return jax.shard_map(
        body,
        mesh=mesh,
        in_specs=placed,
        out_specs=(P("probe", "snp"), P(None, "probe"), P()),
        check_vma=False,
    )
```

profile of v0, /device:TPU:0, one launch (start us, length us, event | category | flops | bytes accessed | tf_op | source)
XLA Modules:
  0.0 129.7 jit_solution(3306518735828132539)
XLA Ops:
  7.2 0.0 reduce-scatter.4.cloned.1.call-start
  7.2 0.7 broadcast_multiply_fusion.1
  7.9 0.0 copy-start.1
  7.9 2.6 %fusion = f32[8,256]{1,0:T(8,128)S(1)} fusion(bf16[8,256]{1,0:T(8,128)(2,1)} %param.5, bf16[256,2048]{1,0:T(8,128)(2,1)} %param.3, f32[2048]{0:T(1024)S(1)} %get-tuple-element.11, f32[2048]{0:T(1024)S(1)} %get-tuple-element.10), kind=kOutput, calls=%fused_computation.3 | convolution fusion | flops 20987904 | bytes 1077248 | tf_op jit(solution)/shard_map/dot_general | solution.py:9
  10.5 23.4 %psum.28 = f32[8,256]{1,0:T(8,128)S(1)} all-reduce(f32[8,256]{1,0:T(8,128)S(1)} %fusion), channel_id=1, replica_groups=mesh['snp'=8,'probe'=4] {'snp'}, use_global_device_ids=true, to_apply=%region_0.0 | all-reduce | flops 2048 | bytes 16384 | tf_op jit(solution)/shard_map/psum | solution.py:25
  34.0 0.0 copy-done.1
  34.0 0.0 copy-start
  34.0 1.3 %convolution_bitcast_fusion = f32[256,8]{1,0:T(8,128)} fusion(bf16[256,2048]{1,0:T(8,128)(2,1)S(1)} %copy-done.1, f32[2048]{0:T(1024)S(1)} %get-tuple-element.11, f32[2048]{0:T(1024)S(1)} %get-tuple-element.10, f32[8,256]{1,0:T(8,128)S(1)} %psum.28), kind=kOutput, calls=%fused_computation.4 | convolution fusion | flops 20992000 | bytes 1081344
  35.3 0.0 reduce-scatter.4.cloned.1.call-update
  35.3 59.6 %reduce-scatter.4.cloned.1.call-done = f32[32,8]{1,0:T(8,128)} async-done(((f32[256,8]{1,0:T(8,128)}), f32[32,8]{1,0:T(8,128)}) %reduce-scatter.4.cloned.1.call-update) | async-done | bytes 1040
  95.0 0.8 copy.7
  95.7 0.0 copy-done
  95.7 0.7 fusion.1
  96.5 19.5 %all-reduce = (f32[1,8]{1,0:T(1,128)S(1)}, f32[1,8]{1,0:T(1,128)S(1)}) all-reduce(f32[1,8]{1,0:T(1,128)S(1)} %get-tuple-element.12, f32[1,8]{1,0:T(1,128)S(1)} %get-tuple-element.13), channel_id=1, replica_groups=mesh['snp'=8,'probe'=4] {'snp'}, use_global_device_ids=true, to_apply=%region_5.0 | all-reduce | flops 16 | bytes 128 | tf_op jit(solution)/shard_map/psum | solution.py:33
  116.0 0.7 fusion.5
  116.7 5.7 %psum.31 = f32[2]{0:T(128)S(1)} all-reduce(f32[2]{0:T(128)S(1)} %get-tuple-element.7), channel_id=1, replica_groups=mesh['snp'=8,'probe'=4] {'probe'}, use_global_device_ids=true, to_apply=%region_7.0 | all-reduce | flops 2 | bytes 16 | tf_op jit(solution)/shard_map/psum | solution.py:35
  122.4 0.5 broadcast_multiply_fusion.3
  (2 shorter events, 0.0 us)
Async XLA Ops:
  7.2 87.8 %reduce-scatter.4.cloned.1.call-start = ((), (), s32[]{:S(2)}) async-start(), calls=%async_computation.1 | async-start | bytes 147456
  7.9 26.0 %copy-start.1 = (bf16[256,2048]{1,0:T(8,128)(2,1)S(1)}, bf16[256,2048]{1,0:T(8,128)(2,1)}, u32[]{:S(2)}) copy-start(bf16[256,2048]{1,0:T(8,128)(2,1)} %param.3) | copy-start | bytes 3145732
  34.0 61.8 %copy-start = (bf16[8,256]{1,0:T(8,128)(2,1)S(1)}, bf16[8,256]{1,0:T(8,128)(2,1)}, u32[]{:S(2)}) copy-start(bf16[8,256]{1,0:T(8,128)(2,1)} %param.5) | copy-start | bytes 12292
Sparse Core Ops, SparseCore 0:
  35.4 59.4 reduce-scatter.3
where the time goes:
time: 130 us
  waiting for transfers between devices  59.6 us (46%)
  blocking collectives  48.6 us (37%)
  between operations  14.1 us (11%)
  matrix products  3.96 us (3%)
  other arithmetic  2.65 us (2%)
    unnamed x2, waiting for transfers between devices  59.6 us
    psum x1, blocking collectives, body(): summed = lax.psum(partial_once, 'snp') / columns  23.4 us
    psum x1, blocking collectives, body(): form_second = lax.psum(local_second, 'snp')  19.5 us
    psum x1, blocking collectives, body(): estimates = lax.psum(jnp.sum(forms, axis=1), 'probe') / probes_all  5.66 us
    dot_general x1, matrix products, apply_columns(): lax.dot_general(projected, standard, (((1,), (1,)), ((), ())), preferred_...  2.63 us
  transfers between devices with their start and end apart: 1, of which 1 were waited for; matrix products, arithmetic and copies ran while one was open for 0% of the time, Pallas kernels for 0%

commit v1 on v0

--- a/solution.py
+++ b/solution.py
@@ -2,6 +2,14 @@
 import jax.numpy as jnp
 from jax import lax
 from jax.sharding import PartitionSpec as P
+
+
+def added_up(shard, axis):
+    devices, summed = (lax.axis_size(axis), shard)
+    for far in [1 << k for k in range(devices.bit_length() - 1)]:
+        route = [(i, i ^ far) for i in range(devices)]
+        summed = summed + lax.ppermute(summed, axis, route)
+    return summed
 
 
 def apply_columns(vectors, standard):
@@ -30,7 +38,7 @@
     partial_twice = apply_columns(kin_round, standard)
     kin_twice = lax.psum_scatter(partial_twice, "snp", scatter_dimension=1, tiled=True) / columns
     local_second = jnp.sum(signs_owned * kin_twice, axis=1) / samples_all
-    form_second = lax.psum(local_second, "snp")
+    form_second = added_up(local_second, "snp")
     forms = jnp.stack([form_first, form_second])
     estimates = lax.psum(jnp.sum(forms, axis=1), "probe") / probes_all
     return (kin_twice, forms, estimates)

time: 130 us -> 140 us (1.077)
  waiting for transfers between devices: 59.6 us -> 67.7 us
  starting transfers between devices: 0.04 us -> 1.59 us
    ppermute x0 -> x3, waiting for transfers between devices: none -> 8.02 us  [added_up(): summed = summed + lax.ppermute(summed, axis, route)]
    ppermute x0 -> x3, starting transfers between devices: none -> 1.56 us  [added_up(): summed = summed + lax.ppermute(summed, axis, route)]
  transfers between devices with their start and end apart: 1 -> 4, of which waited for: 1 -> 3; matrix products, arithmetic and copies ran while one was open for 0% -> 0% of each run, Pallas kernels for 0% -> 0%
where the time goes in v1:
time: 140 us; the launch traced here: 139 us
  waiting for transfers between devices  67.7 us (48%)
  blocking collectives  48.6 us (35%)
  between operations  14.1 us (10%)
  matrix products  3.96 us (3%)
  other arithmetic  2.66 us (2%)
  starting transfers between devices  1.59 us (1%)
    unnamed x2, waiting for transfers between devices  59.6 us
    psum x1, blocking collectives, body(): summed = lax.psum(partial_once, 'snp') / columns  23.4 us
    psum x1, blocking collectives, body(): form_first = lax.psum(local_first, 'snp')  19.5 us
    ppermute x3, waiting for transfers between devices, added_up(): summed = summed + lax.ppermute(summed, axis, route)  8.02 us
    psum x1, blocking collectives, body(): estimates = lax.psum(jnp.sum(forms, axis=1), 'probe') / probes_all  5.66 us
  transfers between devices with their start and end apart: 4, of which 3 were waited for; matrix products, arithmetic and copies ran while one was open for 0% of the time, Pallas kernels for 0%

profile of v1, /device:TPU:0, one launch (start us, length us, event | category | flops | bytes accessed | tf_op | source)
XLA Modules:
  0.0 139.3 jit_solution(8378845515362474365)
XLA Ops:
  7.2 0.0 reduce-scatter.4.cloned.1.call-start
  7.2 0.7 broadcast_multiply_fusion.1
  7.9 0.0 copy-start.1
  7.9 2.6 %fusion = f32[8,256]{1,0:T(8,128)S(1)} fusion(bf16[8,256]{1,0:T(8,128)(2,1)} %param.5, bf16[256,2048]{1,0:T(8,128)(2,1)} %param.3, f32[2048]{0:T(1024)S(1)} %get-tuple-element.9, f32[2048]{0:T(1024)S(1)} %get-tuple-element.8), kind=kOutput, calls=%fused_computation.3 | convolution fusion | flops 20987904 | bytes 1077248 | tf_op jit(solution)/shard_map/dot_general | solution.py:17
  10.5 23.4 %psum.21 = f32[8,256]{1,0:T(8,128)S(1)} all-reduce(f32[8,256]{1,0:T(8,128)S(1)} %fusion), channel_id=1, replica_groups=mesh['snp'=8,'probe'=4] {'snp'}, use_global_device_ids=true, to_apply=%region_0.0 | all-reduce | flops 2048 | bytes 16384 | tf_op jit(solution)/shard_map/psum | solution.py:33
  34.0 0.0 copy-done.1
  34.0 0.0 copy-start
  34.0 1.3 convolution_bitcast_fusion
  35.3 0.0 reduce-scatter.4.cloned.1.call-update
  35.3 59.6 %reduce-scatter.4.cloned.1.call-done = f32[32,8]{1,0:T(8,128)} async-done(((f32[256,8]{1,0:T(8,128)}), f32[32,8]{1,0:T(8,128)}) %reduce-scatter.4.cloned.1.call-update) | async-done | bytes 1040
  95.0 0.8 copy.7
  95.7 0.0 copy-done
  95.7 0.7 fusion.1
  96.5 1.5 %collective-permute-start = (f32[8]{0:T(128)S(1)}, f32[8]{0:T(128)S(1)}, u32[]{:S(2)}, u32[]{:S(2)}) collective-permute-start(f32[8]{0:T(128)S(1)} %broadcast_multiply_fusion.4), channel_id=1, source_target_pairs={{0,4},{4,0},{8,12},{12,8},{16,20},{20,16},{24,28},{28,24},{1,5},{5... | collective-permute-start | bytes 104 | tf_op jit(solution)/shard_map/ppermute | solution.py:11
  98.0 19.5 %psum.22 = f32[1,8]{1,0:T(1,128)S(1)} all-reduce(f32[1,8]{1,0:T(1,128)S(1)} %multiply_bitcast_fusion), channel_id=1, replica_groups=mesh['snp'=8,'probe'=4] {'snp'}, use_global_device_ids=true, to_apply=%region_3.0 | all-reduce | flops 8 | bytes 64 | tf_op jit(solution)/shard_map/psum | solution.py:37
  117.5 0.0 collective-permute-done
  117.5 0.1 collective-permute-start.1
  117.6 3.6 %collective-permute-done.1 = f32[8]{0:T(128)S(1)} collective-permute-done((f32[8]{0:T(128)S(1)}, f32[8]{0:T(128)S(1)}, u32[]{:S(2)}, u32[]{:S(2)}) %collective-permute-start.1) | collective-permute-done | bytes 64 | tf_op jit(solution)/shard_map/ppermute | solution.py:11
  121.2 0.0 collective-permute-start.2
  121.2 4.5 %collective-permute-done.2 = f32[8]{0:T(128)S(1)} collective-permute-done((f32[8]{0:T(128)S(1)}, f32[8]{0:T(128)S(1)}, u32[]{:S(2)}, u32[]{:S(2)}) %collective-permute-start.2) | collective-permute-done | bytes 64 | tf_op jit(solution)/shard_map/ppermute | solution.py:11
  125.6 0.7 fusion.6
  126.3 5.7 %psum.23 = f32[2]{0:T(128)S(1)} all-reduce(f32[2]{0:T(128)S(1)} %get-tuple-element.5), channel_id=1, replica_groups=mesh['snp'=8,'probe'=4] {'probe'}, use_global_device_ids=true, to_apply=%region_6.0 | all-reduce | flops 2 | bytes 16 | tf_op jit(solution)/shard_map/psum | solution.py:43
  132.0 0.5 broadcast_multiply_fusion.3
  (6 shorter events, 0.0 us)
Async XLA Ops:
  7.2 87.8 %reduce-scatter.4.cloned.1.call-start = ((), (), s32[]{:S(2)}) async-start(), calls=%async_computation.1 | async-start | bytes 147456
  7.9 26.0 %copy-start.1 = (bf16[256,2048]{1,0:T(8,128)(2,1)S(1)}, bf16[256,2048]{1,0:T(8,128)(2,1)}, u32[]{:S(2)}) copy-start(bf16[256,2048]{1,0:T(8,128)(2,1)} %param.3) | copy-start | bytes 3145732
  34.0 61.8 %copy-start = (bf16[8,256]{1,0:T(8,128)(2,1)S(1)}, bf16[8,256]{1,0:T(8,128)(2,1)}, u32[]{:S(2)}) copy-start(bf16[8,256]{1,0:T(8,128)(2,1)} %param.5) | copy-start | bytes 12292
  96.5 21.0 %collective-permute-start = (f32[8]{0:T(128)S(1)}, f32[8]{0:T(128)S(1)}, u32[]{:S(2)}, u32[]{:S(2)}) collective-permute-start(f32[8]{0:T(128)S(1)} %broadcast_multiply_fusion.4), channel_id=1, source_target_pairs={{0,4},{4,0},{8,12},{12,8},{16,20},{20,16},{24,28},{28,24},{1,5},{5... | collective-permute-start | bytes 104 | tf_op jit(solution)/shard_map/ppermute | solution.py:11
  117.5 3.6 %collective-permute-start.1 = (f32[8]{0:T(128)S(1)}, f32[8]{0:T(128)S(1)}, u32[]{:S(2)}, u32[]{:S(2)}) collective-permute-start(f32[8]{0:T(128)S(1)} %fusion.5), channel_id=1, source_target_pairs={{0,8},{4,12},{8,0},{12,4},{16,24},{20,28},{24,16},{28,20},{1,9},{5... | collective-permute-start | bytes 104 | tf_op jit(solution)/shard_map/ppermute | solution.py:11
  121.2 4.5 %collective-permute-start.2 = (f32[8]{0:T(128)S(1)}, f32[8]{0:T(128)S(1)}, u32[]{:S(2)}, u32[]{:S(2)}) collective-permute-start(f32[8]{0:T(128)S(1)} %add.23), channel_id=1, source_target_pairs={{0,16},{4,20},{8,24},{12,28},{16,0},{20,4},{24,8},{28,12},{1,17},{... | collective-permute-start | bytes 104 | tf_op jit(solution)/shard_map/ppermute | solution.py:11
Sparse Core Ops, SparseCore 0:
  35.4 59.4 reduce-scatter.3
